TPU v7x, 32 devices: a whole 2x2x4 slice. The times are simulated.
32 devices in a mesh: groups: 2 (over y), dp: 4 (over z), section: 2 (over x), tensor: 2 (over core).
Axes of the slice: x: 2, y: 2, z: 4, core: 2. Of those that a mesh axis runs over, the one named last changes fastest.
Arguments:
- hidden: bfloat16 [128, 8, 5120], P(('groups', 'dp')), parts along dimension 0, may hold values from -6 to 6
- unembed: bfloat16 [128, 8, 5120], P(('groups', 'dp')), parts along dimension 0, may hold values from -0.02734375 to 0.02734375
- value_proj: bfloat16 [2, 5120, 512], P('section', 'dp', 'tensor'), may hold values from -0.078125 to 0.078125
- output_proj: bfloat16 [2, 512, 5120], P('section', 'tensor', 'dp'), may hold values from -0.125 to 0.125
- norm_gains: float32 [2, 5120], P('section'), may hold values from 0.1 to 1.9
- survive: int32 [8], P(('groups', 'dp')), parts along dimension 0, may hold values from 0 to 1, as said below
- lengths: int32 [128], P(('groups', 'dp')), parts along dimension 0, may hold values from 1 to 8
- assign: int32 [128], P(('groups', 'dp')), parts along dimension 0, may hold values from 0 to 16, as said below
- advantage: float32 [128], P(('groups', 'dp')), parts along dimension 0, may hold values from -4 to 4
- reference_logit: float32 [128, 8], P(('groups', 'dp')), parts along dimension 0, may hold values from -4 to 4
- recorded_gap: float32 [128, 8], P(('groups', 'dp')), parts along dimension 0, may hold values from -2 to 2
Outputs:
- grad_value: float32 [4, 5120, 512], P(('groups', 'section'), 'dp', 'tensor'), parts along dimension 0
- grad_output: float32 [4, 512, 5120], P(('groups', 'section'), 'tensor', 'dp'), parts along dimension 0
There are 2 independent parts, one for each index of `groups`. A program takes and returns all parts, laid end to end along the dimension named above; an argument that names none is the same for every part. Nothing has to cross between parts.
Inputs may be any that keep to these rules, and one draw needn't show every extreme that they name: `survive`: 1 where the group of 16 responses is kept, 0 where it is dropped; in every draw all groups of some dp index are kept. `assign`: the 16 slots of a dp index list the local positions (0 to 15) of the responses of its kept groups, each exactly once, then hold 16 in every other slot.
All inputs are finite; a program needn't handle non-finite values.
Results may differ from a plain program's by a relative error of at most 0.029.
Values may be sent and summed in bfloat16 or wider, within the bound.
A program may use at most 64 MiB of HBM per device.

v0:
```python
import math

import jax
import jax.numpy as jnp
from jax import lax
from jax.sharding import PartitionSpec as P

GROUP = 16
MB_RESP = 8


eps_norm = 1e-06
loss_scale = 4096.0
clip_high = math.log(1.28)
clip_low = math.log(0.8)


def from_behind(block, axis, distance):
    devices = range(lax.axis_size(axis))
    route = [(i - distance, i) for i in devices if i - distance in devices]
    return lax.ppermute(block, axis, route)


def norm_forward(row_block, norm_gain):
    values = row_block.astype(jnp.float32)
    inverse = lax.rsqrt(jnp.mean(values * values, axis=-1, keepdims=True) + eps_norm)
    return (values, inverse, (values * inverse * norm_gain).astype(jnp.bfloat16))


def norm_backward(values, inverse, norm_gain, upstream):
    scaled = upstream * norm_gain
    inner_sum = jnp.sum(scaled * values, axis=-1, keepdims=True) / values.shape[-1]
    return inverse * scaled - values * (inverse * inverse * inverse) * inner_sum


def contract_last(left_rows, right_rows):
    return lax.dot_general(
        left_rows, right_rows, (((1,), (1,)), ((), ())), preferred_element_type=jnp.float32
    )


def contract_first(left_rows, right_rows):
    return lax.dot_general(
        left_rows, right_rows, (((0,), (0,)), ((), ())), preferred_element_type=jnp.float32
    )


def take_slot(slot_store, slot_index):
    return lax.dynamic_index_in_dim(slot_store, slot_index, 0, keepdims=False)


def put_slot(slot_store, new_value, slot_index, active):
    previous = take_slot(slot_store, slot_index)
    return lax.dynamic_update_index_in_dim(
        slot_store, jnp.where(active, new_value, previous), slot_index, 0
    )


def local(
    hidden,
    unembed,
    value_proj,
    output_proj,
    norm_gains,
    survive,
    lengths,
    assign,
    advantage,
    reference_logit,
    recorded_gap,
):
    resp_count = hidden.shape[0]
    positions = hidden.shape[1]
    model_width = hidden.shape[2]
    half_value = value_proj.shape[2]
    micro_count = resp_count // MB_RESP
    row_count = MB_RESP * positions
    section_count = lax.axis_size("section")
    section_index = lax.axis_index("section")
    is_last = section_index == section_count - 1
    norm_gain = norm_gains[0]
    alive_mask = jnp.repeat(survive, GROUP)
    local_count = jnp.sum((alive_mask * lengths).astype(jnp.float32))
    gathered_value, gathered_output = (
        lax.all_gather(value_proj, "dp", axis=1, tiled=True),
        lax.all_gather(output_proj, "dp", axis=2, tiled=True),
    )
    w_first = gathered_value[0]
    w_second = gathered_output[0]

    def pick(array):
        return jnp.take(array, assign, axis=0, mode="fill", fill_value=0)

    slot_hidden = pick(hidden).reshape(micro_count, row_count, model_width)
    slot_unembed = pick(unembed).reshape(micro_count, row_count, model_width)
    position_index = lax.broadcasted_iota(jnp.int32, (resp_count, positions), 1)
    live_mask = (position_index < pick(lengths)[:, None]).astype(jnp.float32)
    advantages = jnp.broadcast_to(pick(advantage)[:, None], (resp_count, positions))
    gap_rows = pick(recorded_gap)
    clipped = (advantages > 0) & (gap_rows > clip_high) | (advantages < 0) & (gap_rows < clip_low)
    kept_mask = 1.0 - clipped.astype(jnp.float32)
    weight_rows = (-loss_scale * advantages * kept_mask * live_mask).reshape(micro_count, row_count)
    logit_base = pick(reference_logit).reshape(micro_count, row_count)
    step_count = micro_count + section_count - 1
    store_in = jnp.zeros((micro_count, row_count, model_width), jnp.bfloat16)
    store_normed = jnp.zeros((micro_count, row_count, model_width), jnp.bfloat16)
    store_projected = jnp.zeros((micro_count, row_count, half_value), jnp.bfloat16)
    store_out = jnp.zeros((micro_count, row_count, model_width), jnp.bfloat16)
    arriving = jnp.zeros((row_count, model_width), jnp.bfloat16)
    for step_index in range(step_count):
        micro_index = step_index - section_index
        active = (micro_index >= 0) & (micro_index < micro_count)
        clamped = jnp.clip(micro_index, 0, micro_count - 1)
        entering = jnp.where(section_index == 0, take_slot(slot_hidden, clamped), arriving)
        values, inverse, normed = norm_forward(entering, norm_gain)
        projected = jnp.dot(normed, w_first, preferred_element_type=jnp.float32).astype(
            jnp.bfloat16
        )
        partial_out = jnp.dot(projected, w_second, preferred_element_type=jnp.float32)
        mixed_sum = lax.psum(partial_out.astype(jnp.bfloat16), "tensor").astype(jnp.float32)
        leaving = (values + mixed_sum).astype(jnp.bfloat16)
        store_in = put_slot(store_in, entering, clamped, active)
        store_normed = put_slot(store_normed, normed, clamped, active)
        store_projected = put_slot(store_projected, projected, clamped, active)
        store_out = put_slot(store_out, leaving, clamped, active)
        arriving = from_behind(leaving, "section", 1)
    store_upstream = jnp.zeros((micro_count, row_count, model_width), jnp.bfloat16)
    store_grad_value = jnp.zeros((micro_count, row_count, half_value), jnp.bfloat16)
    arriving = jnp.zeros((row_count, model_width), jnp.bfloat16)
    for step_index in range(step_count):
        micro_index = step_index - (section_count - 1 - section_index)
        active = (micro_index >= 0) & (micro_index < micro_count)
        clamped = jnp.clip(micro_index, 0, micro_count - 1)
        top_rows = take_slot(store_out, clamped).astype(jnp.float32)
        unembed_rows = take_slot(slot_unembed, clamped).astype(jnp.float32)
        logit = jnp.sum(top_rows * unembed_rows, axis=-1)
        seed_rows = take_slot(weight_rows, clamped) * jnp.exp(
            logit - take_slot(logit_base, clamped)
        )
        start_grad = (seed_rows[:, None] * unembed_rows).astype(jnp.bfloat16)
        upstream = jnp.where(is_last, start_grad, arriving)
        entering = take_slot(store_in, clamped)
        normed = take_slot(store_normed, clamped)
        projected = take_slot(store_projected, clamped)
        grad_projected = contract_last(upstream, w_second).astype(jnp.bfloat16)
        partial_norm = contract_last(grad_projected, w_first)
        grad_normed = lax.psum(partial_norm.astype(jnp.bfloat16), "tensor").astype(jnp.float32)
        values, inverse, unused_normed = norm_forward(entering, norm_gain)
        grad_entering = (
            upstream.astype(jnp.float32) + norm_backward(values, inverse, norm_gain, grad_normed)
        ).astype(jnp.bfloat16)
        store_upstream = put_slot(store_upstream, upstream, clamped, active)
        store_grad_value = put_slot(store_grad_value, grad_projected, clamped, active)
        arriving = from_behind(grad_entering, "section", -1)
    flat_normed = store_normed.reshape(micro_count * row_count, model_width)
    flat_upstream = store_upstream.reshape(micro_count * row_count, model_width)
    flat_grad_value = store_grad_value.reshape(micro_count * row_count, half_value)
    flat_projected = store_projected.reshape(micro_count * row_count, half_value)
    reduced = lax.psum_scatter(
        jnp.concatenate(
            [
                contract_first(flat_normed, flat_grad_value),
                contract_first(flat_upstream, flat_projected),
            ],
            axis=1,
        ).astype(jnp.bfloat16),
        "dp",
        scatter_dimension=0,
        tiled=True,
    ).astype(jnp.float32)
    token_total = lax.psum(local_count, "dp")
    scaled_grads = reduced / token_total
    grad_value = scaled_grads[:, :half_value][None]
    grad_output = scaled_grads[:, half_value:].T[None]
    return (grad_value, grad_output)


def solution(mesh):
    placed = (
        P(("groups", "dp"), None, None),
        P(("groups", "dp"), None, None),
        P("section", "dp", "tensor"),
        P("section", "tensor", "dp"),
        P("section", None),
        P(("groups", "dp")),
        P(("groups", "dp")),
        P(("groups", "dp")),
        P(("groups", "dp")),
        P(("groups", "dp"), None),
        P(("groups", "dp"), None),
    )
    return jax.shard_map(
        local,
        mesh=mesh,
        in_specs=placed,
        out_specs=(
            P(("groups", "section"), "dp", "tensor"),
            P(("groups", "section"), "tensor", "dp"),
        ),
        check_vma=False,
    )
```

profile of v0, /device:TPU:0, one launch (start us, length us, event | category | flops | bytes accessed | tf_op | source)
XLA Modules:
  0.0 449.3 jit_solution(629598408572374933)
XLA Ops:
  9.5 1.7 gather_fusion.2
  11.2 1.7 gather_fusion.4
  14.8 2.0 broadcast_select_fusion.1
  18.2 48.9 %all-gather.3.cloned.1.call-done = bf16[1,5120,256]{2,1,0:T(8,128)(2,1)} async-done(((bf16[1,1280,256]{2,1,0:T(8,128)(2,1)}), bf16[1,5120,256]{2,1,0:T(8,128)(2,1)}) %all-gather.3.cloned.1.call-update) | async-done | bytes 2621456 | tf_op jit(solution)/shard_map/all_gather | solution.py:85
  67.1 2.6 bitcast_dynamic-update-slice_fusion.10
  69.7 52.5 %all-gather.5.cloned.1.call-done = bf16[1,256,5120]{2,1,0:T(8,128)(2,1)} async-done(((bf16[1,256,1280]{2,1,0:T(8,128)(2,1)}), bf16[1,256,5120]{2,1,0:T(8,128)(2,1)}) %all-gather.5.cloned.1.call-update) | async-done | bytes 2621456 | tf_op jit(solution)/shard_map/all_gather | solution.py:86
  122.2 3.2 convolution_convert_fusion.4
  125.7 1.2 broadcast.209.clone
  128.5 14.6 %all-reduce.6.cloned.1.call-done = bf16[64,5120]{1,0:T(8,128)(2,1)} async-done(((bf16[64,5120]{1,0:T(8,128)(2,1)}), bf16[64,5120]{1,0:T(8,128)(2,1)}) %all-reduce.6.cloned.1.call-update) | async-done | bytes 655376 | tf_op jit(solution)/shard_map/psum | solution.py:120
  143.2 1.2 copy-done.14
  144.4 1.4 bitcast_dynamic-update-slice_fusion.5
  145.8 3.7 collective-permute-start
  150.7 13.2 %collective-permute-done = bf16[64,5120]{1,0:T(8,128)(2,1)S(1)} collective-permute-done((bf16[64,5120]{1,0:T(8,128)(2,1)S(1)}, bf16[64,5120]{1,0:T(8,128)(2,1)S(1)}, u32[]{:S(2)}, u32[]{:S(2)}) %collective-permute-start) | collective-permute-done | bytes 655392 | tf_op jit(solution)/shard_map/ppermute | solution.py:21
  167.0 1.5 convolution_convert_fusion.3
  168.6 2.0 constant_dynamic-slice_fusion.14
  170.6 2.0 constant_dynamic-slice_fusion.8
  172.6 16.8 %all-reduce.8.cloned.1.call-done = bf16[64,5120]{1,0:T(8,128)(2,1)} async-done(((bf16[64,5120]{1,0:T(8,128)(2,1)}), bf16[64,5120]{1,0:T(8,128)(2,1)}) %all-reduce.8.cloned.1.call-update) | async-done | bytes 655376 | tf_op jit(solution)/shard_map/psum | solution.py:120
  189.4 2.5 bitcast_dynamic-update-slice_fusion.4
  191.9 3.7 collective-permute-start.1
  195.6 2.2 constant_dynamic-slice_fusion.13
  197.8 12.1 %collective-permute-done.1 = bf16[64,5120]{1,0:T(8,128)(2,1)S(1)} collective-permute-done((bf16[64,5120]{1,0:T(8,128)(2,1)S(1)}, bf16[64,5120]{1,0:T(8,128)(2,1)S(1)}, u32[]{:S(2)}, u32[]{:S(2)}) %collective-permute-start.1) | collective-permute-done | bytes 655392 | tf_op jit(solution)/shard_map/ppermute | solution.py:21
  210.1 1.4 bitcast_dynamic-update-slice_fusion.2
  213.9 1.4 convolution_convert_fusion.2
  215.4 1.2 constant_dynamic-slice_fusion.17
  219.3 17.0 %all-reduce.10.cloned.1.call-done = bf16[64,5120]{1,0:T(8,128)(2,1)} async-done(((bf16[64,5120]{1,0:T(8,128)(2,1)}), bf16[64,5120]{1,0:T(8,128)(2,1)}) %all-reduce.10.cloned.1.call-update) | async-done | bytes 655376 | tf_op jit(solution)/shard_map/psum | solution.py:120
  236.2 3.1 bitcast_dynamic-update-slice_fusion.6
  239.3 2.4 fusion.32
  243.5 1.7 convolution_convert_fusion.1
  247.6 17.8 %all-reduce.12.cloned.1.call-done = bf16[64,5120]{1,0:T(8,128)(2,1)} async-done(((bf16[64,5120]{1,0:T(8,128)(2,1)}), bf16[64,5120]{1,0:T(8,128)(2,1)}) %all-reduce.12.cloned.1.call-update) | async-done | bytes 655376 | tf_op jit(solution)/shard_map/psum | solution.py:147
  265.4 2.1 fusion.48
  267.6 1.6 fusion.46
  269.2 1.5 collective-permute-start.2
  271.8 16.1 %collective-permute-done.2 = bf16[64,5120]{1,0:T(8,128)(2,1)S(1)} collective-permute-done((bf16[64,5120]{1,0:T(8,128)(2,1)S(1)}, bf16[64,5120]{1,0:T(8,128)(2,1)S(1)}, u32[]{:S(2)}, u32[]{:S(2)}) %collective-permute-start.2) | collective-permute-done | bytes 655392 | tf_op jit(solution)/shard_map/ppermute | solution.py:21
  288.0 1.2 bitcast_dynamic-update-slice_fusion.1
  291.7 1.7 convolution_convert_fusion
  293.5 19.2 %all-reduce.14.cloned.1.call-done = bf16[64,5120]{1,0:T(8,128)(2,1)} async-done(((bf16[64,5120]{1,0:T(8,128)(2,1)}), bf16[64,5120]{1,0:T(8,128)(2,1)}) %all-reduce.14.cloned.1.call-update) | async-done | bytes 655376 | tf_op jit(solution)/shard_map/psum | solution.py:147
  312.7 1.7 fusion.53
  314.4 1.7 fusion.52
  316.1 1.3 collective-permute-start.3
  318.6 16.3 %collective-permute-done.3 = bf16[64,5120]{1,0:T(8,128)(2,1)S(1)} collective-permute-done((bf16[64,5120]{1,0:T(8,128)(2,1)S(1)}, bf16[64,5120]{1,0:T(8,128)(2,1)S(1)}, u32[]{:S(2)}, u32[]{:S(2)}) %collective-permute-start.3) | collective-permute-done | bytes 655392 | tf_op jit(solution)/shard_map/ppermute | solution.py:21
  337.1 1.2 bitcast_dynamic-update-slice_fusion
  338.3 2.2 fusion.1
  340.5 2.7 pad_maximum_fusion
  344.5 12.9 %psum.47 = f32[]{:T(128)} all-reduce(f32[]{:T(128)} %convert_reduce_fusion), channel_id=1, replica_groups=mesh['groups'=2,'dp'=4,'section'=2,'tensor'=2] {'dp'}, use_global_device_ids=true, to_apply=%region_17.20 | all-reduce | flops 1 | bytes 8 | tf_op jit(solution)/shard_map/psum | solution.py:171
  357.4 80.2 %reduce-scatter.2.cloned.1.call-done = bf16[1280,512]{0,1:T(8,128)(2,1)} async-done(((bf16[5120,512]{0,1:T(8,128)(2,1)}), bf16[1280,512]{0,1:T(8,128)(2,1)}) %reduce-scatter.2.cloned.1.call-update) | async-done | bytes 1310736 | tf_op jit(solution)/shard_map/reduce_scatter | solution.py:159
  437.6 2.2 convert_divide_fusion
  439.7 1.2 slice_bitcast_fusion
  441.0 1.5 copy.18
  (126 shorter events, 28.8 us)
Async XLA Ops:
  7.2 2.3 copy-start
  7.2 1.6 copy-start.30
  7.2 1.6 copy-start.1
  7.2 59.9 %all-gather.3.cloned.1.call-start = ((), (), s32[]{:S(2)}) async-start(), calls=%async_computation.1 | async-start | bytes 3276800 | tf_op jit(solution)/shard_map/all_gather | solution.py:85
  7.9 114.3 %all-gather.5.cloned.1.call-start = ((), (), s32[]{:S(2)}) async-start(), calls=%async_computation.2 | async-start | bytes 3276800 | tf_op jit(solution)/shard_map/all_gather | solution.py:86
  8.7 134.4 %all-reduce.6.cloned.1.call-start = ((), (), s32[]{:S(2)}) async-start(), calls=%async_computation.3 | async-start | bytes 1310720 | tf_op jit(solution)/shard_map/psum | solution.py:120
  9.5 1.7 copy-start.27
  11.2 1.7 copy-start.2
  11.2 2.4 copy-start.28
  11.2 3.0 copy-start.29
  14.8 52.3 %copy-start.26 = (f32[1,5120]{1,0:T(1,128)S(1)}, f32[1,5120]{1,0:T(1,128)}, u32[]{:S(2)}) copy-start(f32[1,5120]{1,0:T(1,128)} %param.19) | copy-start | bytes 61444
  16.8 1.1 copy-start.12
  125.4 64.0 %all-reduce.8.cloned.1.call-start = ((), (), s32[]{:S(2)}) async-start(), calls=%async_computation.4 | async-start | bytes 1310720 | tf_op jit(solution)/shard_map/psum | solution.py:120
  125.7 1.8 copy-start.13
  143.1 1.3 copy-start.14
  145.8 4.9 %copy-start.20 = (bf16[2,64,5120]{2,1,0:T(8,128)(2,1)}, bf16[2,64,5120]{2,1,0:T(8,128)(2,1)S(1)}, u32[]{:S(2)}) copy-start(bf16[2,64,5120]{2,1,0:T(8,128)(2,1)S(1)} %get-tuple-element.22) | copy-start | bytes 3932164
  145.8 18.1 %collective-permute-start = (bf16[64,5120]{1,0:T(8,128)(2,1)S(1)}, bf16[64,5120]{1,0:T(8,128)(2,1)S(1)}, u32[]{:S(2)}, u32[]{:S(2)}) collective-permute-start(bf16[64,5120]{1,0:T(8,128)(2,1)S(1)} %get-tuple-element.23), channel_id=1, source_target_pairs={{0,2},{1,3},{4,6},{5,7},{8,10},{9,11},{12,14},{13,15},{16,18},{17,... | collective-permute-start | bytes 1966088 | tf_op jit(solution)/shard_map/ppermute | solution.py:21
  150.7 14.6 %copy-start.8 = (bf16[1,5120,256]{2,1,0:T(8,128)(2,1)S(1)}, bf16[1,5120,256]{2,1,0:T(8,128)(2,1)}, u32[]{:S(2)}) copy-start(bf16[1,5120,256]{2,1,0:T(8,128)(2,1)} %all-gather.3.cloned.1.call-done) | copy-start | bytes 7864324
  165.3 1.7 copy-start.3
  168.5 67.7 %all-reduce.10.cloned.1.call-start = ((), (), s32[]{:S(2)}) async-start(), calls=%async_computation.5 | async-start | bytes 1310720 | tf_op jit(solution)/shard_map/psum | solution.py:120
  191.9 18.1 %collective-permute-start.1 = (bf16[64,5120]{1,0:T(8,128)(2,1)S(1)}, bf16[64,5120]{1,0:T(8,128)(2,1)S(1)}, u32[]{:S(2)}, u32[]{:S(2)}) collective-permute-start(bf16[64,5120]{1,0:T(8,128)(2,1)S(1)} %get-tuple-element.21), channel_id=1, source_target_pairs={{0,2},{1,3},{4,6},{5,7},{8,10},{9,11},{12,14},{13,15},{16,18},{17,... | collective-permute-start | bytes 1966088 | tf_op jit(solution)/shard_map/ppermute | solution.py:21
  195.6 14.5 %copy-start.15 = (bf16[16,8,5120]{2,1,0:T(8,128)(2,1)S(1)}, bf16[16,8,5120]{2,1,0:T(8,128)(2,1)}, u32[]{:S(2)}) copy-start(bf16[16,8,5120]{2,1,0:T(8,128)(2,1)} %copy-done.12) | copy-start | bytes 3932164
  195.6 14.5 %copy-start.25 = (bf16[1,64,5120]{2,1,0:T(8,128)(2,1)S(1)}, bf16[1,64,5120]{2,1,0:T(8,128)(2,1)}, u32[]{:S(2)}) copy-start(bf16[1,64,5120]{2,1,0:T(8,128)(2,1)} %constant_dynamic-slice_fusion.8) | copy-start | bytes 1966084
  210.1 2.0 copy-start.9
  211.5 1.2 copy-start.16
  211.5 1.3 copy-start.21
  212.0 1.9 copy-start.4
  215.4 50.0 %all-reduce.12.cloned.1.call-start = ((), (), s32[]{:S(2)}) async-start(), calls=%async_computation.6 | async-start | bytes 1310720 | tf_op jit(solution)/shard_map/psum | solution.py:147
  215.4 1.5 copy-start.17
  217.3 1.1 copy-start.18
  218.4 17.8 %copy-start.22 = (bf16[64,5120]{1,0:T(8,128)(2,1)S(1)}, bf16[64,5120]{1,0:T(8,128)(2,1)}, u32[]{:S(2)}) copy-start(bf16[64,5120]{1,0:T(8,128)(2,1)} %copy-done.21) | copy-start | bytes 1966084
  239.3 2.4 copy-start.5
  241.8 1.7 copy-start.10
  245.3 67.4 %all-reduce.14.cloned.1.call-start = ((), (), s32[]{:S(2)}) async-start(), calls=%async_computation.7 | async-start | bytes 1310720 | tf_op jit(solution)/shard_map/psum | solution.py:147
  265.4 2.1 copy-start.24
  269.2 18.8 %collective-permute-start.2 = (bf16[64,5120]{1,0:T(8,128)(2,1)S(1)}, bf16[64,5120]{1,0:T(8,128)(2,1)S(1)}, u32[]{:S(2)}, u32[]{:S(2)}) collective-permute-start(bf16[64,5120]{1,0:T(8,128)(2,1)S(1)} %fusion.46), channel_id=1, source_target_pairs={{2,0},{3,1},{6,4},{7,5},{10,8},{11,9},{14,12},{15,13},{18,16},{19,... | collective-permute-start | bytes 1966088 | tf_op jit(solution)/shard_map/ppermute | solution.py:21
  288.0 2.0 copy-start.6
  290.0 1.7 copy-start.11
  293.5 144.1 %reduce-scatter.2.cloned.1.call-start = ((), (), s32[]{:S(2)}) async-start(), calls=%async_computation.8 | async-start | bytes 6553600 | tf_op jit(solution)/shard_map/reduce_scatter | solution.py:159
  312.7 1.7 copy-start.23
  314.4 20.5 %copy-start.7 = (bf16[1,256,5120]{2,1,0:T(8,128)(2,1)S(1)}, bf16[1,256,5120]{2,1,0:T(8,128)(2,1)}, u32[]{:S(2)}) copy-start(bf16[1,256,5120]{2,1,0:T(8,128)(2,1)} %all-gather.5.cloned.1.call-done) | copy-start | bytes 7864324
  316.1 18.8 %collective-permute-start.3 = (bf16[64,5120]{1,0:T(8,128)(2,1)S(1)}, bf16[64,5120]{1,0:T(8,128)(2,1)S(1)}, u32[]{:S(2)}, u32[]{:S(2)}) collective-permute-start(bf16[64,5120]{1,0:T(8,128)(2,1)S(1)} %fusion.52), channel_id=1, source_target_pairs={{2,0},{3,1},{6,4},{7,5},{10,8},{11,9},{14,12},{15,13},{18,16},{19,... | collective-permute-start | bytes 1966088 | tf_op jit(solution)/shard_map/ppermute | solution.py:21
  334.9 1.3 copy-start.19
Sparse Core Ops, SparseCore 0:
  9.6 57.4 all-gather.2
  68.6 53.4 all-gather.4
  125.5 17.5 all-reduce.5
  168.6 20.6 all-reduce.7
  215.5 20.6 all-reduce.9
  245.4 19.9 all-reduce.11
  293.6 19.0 all-reduce.13
  343.3 94.1 reduce-scatter.1
where the time goes:
time: 450 us; the launch traced here: 449 us
  waiting for transfers between devices  326 us (72%)
  local copies, waits for them, and re-layouts  32.9 us (7%)
  other arithmetic  32.2 us (7%)
  matrix products  19.3 us (4%)
  between operations  15.3 us (3%)
  blocking collectives  12.9 us (3%)
  starting transfers between devices  10.5 us (2%)
    reduce_scatter x1, waiting for transfers between devices, local(): lax.psum_scatter(jnp.concatenate([contract_first(flat_normed, flat_grad_v...  80.2 us
    ppermute x4, waiting for transfers between devices, from_behind(): return lax.ppermute(block, axis, route)  57.8 us
    all_gather x1, waiting for transfers between devices, local(): lax.all_gather(output_proj, 'dp', axis=2, tiled=True)  52.5 us
    all_gather x1, waiting for transfers between devices, local(): lax.all_gather(value_proj, 'dp', axis=1, tiled=True)  48.9 us
    psum x3, waiting for transfers between devices, local(): lax.psum(partial_out.astype(jnp.bfloat16), 'tensor').astype(jnp.float32)  48.4 us
    psum x2, waiting for transfers between devices, local(): lax.psum(partial_norm.astype(jnp.bfloat16), 'tensor').astype(jnp.float32)  37 us
    dynamic_update_slice x10, other arithmetic, put_slot(): lax.dynamic_update_index_in_dim(slot_store, jnp.where(active, new_value,...  14.3 us
    psum x1, blocking collectives, local(): token_total = lax.psum(local_count, 'dp')  12.9 us
  transfers between devices with their start and end apart: 12, of which 12 were waited for; matrix products, arithmetic and copies ran while one was open for 6% of the time, Pallas kernels for 0%

commit v1 on v0

v1 whole, which is shorter than its diff:
```python
import functools
import math

import jax
import jax.numpy as jnp
from jax import lax
from jax.experimental import pallas as pl
from jax.experimental.pallas import tpu as pltpu
from jax.sharding import PartitionSpec as P

eps_norm = 1e-06
loss_scale = 4096.0
clip_high = math.log(1.28)
clip_low = math.log(0.8)
LANES = 128
KINDS = ("a", "xf", "uf", "p", "q", "pj", "pjf", "gq", "gqf", "sc", "tk", "x", "g", "w", "e")
BF = jnp.bfloat16
F32 = jnp.float32


def dot(a, b, ca=1, cb=0):
    return lax.dot_general(a, b, (((ca,), (cb,)), ((), ())), preferred_element_type=F32)


def halves(value):
    high = value.astype(BF)
    return high, (value - high.astype(F32)).astype(BF)


def kernel(
    n, sections, width,
    src, w1, w2, gain, rinfo, tok,
    dw1, dw2,
    xs, us, xg, pb, pr, qb, qr, pj, gq, sc, w1o, w2o, yx, yg, tk, exs, exr, pacc, qacc, rkeep,
    ss, rs,
):
    j = lax.axis_index("dp")
    s = lax.axis_index("section")
    t = lax.axis_index("tensor")
    o = 1 - t
    rows = src.shape[1]
    v = w1.shape[2]
    last = sections - 1
    partner = {"tensor": o}

    def blk(b):
        return pl.ds(pl.multiple_of(b * rows, rows), rows)

    def peer(k):
        return lax.rem(j + k, n)

    def send(kind, si, ri, a, b, dev):
        k = KINDS.index(kind)
        pltpu.make_async_remote_copy(
            src_ref=a, dst_ref=b, send_sem=ss.at[k, si], recv_sem=rs.at[k, ri],
            device_id=dev, device_id_type=pl.DeviceIdType.MESH,
        ).start()

    def handle(kind, i, a):
        k = KINDS.index(kind)
        return pltpu.make_async_remote_copy(
            src_ref=a, dst_ref=a, send_sem=ss.at[k, i], recv_sem=rs.at[k, i],
            device_id=partner, device_id_type=pl.DeviceIdType.MESH,
        )

    def got(kind, i, a):
        handle(kind, i, a).wait_recv()

    def sent(kind, i, a):
        handle(kind, i, a).wait_send()

    def others(body):
        def step(k, carry):
            body(peer(k))
            return carry
        lax.fori_loop(1, n, step, 0)

    def everyone(body):
        def step(k, carry):
            body(peer(k))
            return carry
        lax.fori_loop(0, n, step, 0)

    barrier = pltpu.get_barrier_semaphore()

    def greet(dev):
        pl.semaphore_signal(barrier, inc=1, device_id=dev, device_id_type=pl.DeviceIdType.MESH)

    for k in range(1, n):
        greet({"dp": peer(k)})
    greet(partner)

    @pl.when(s > 0)
    def _():
        greet({"section": s - 1})

    @pl.when(s < last)
    def _():
        greet({"section": s + 1})

    pl.semaphore_wait(barrier, n + jnp.where(s > 0, 1, 0) + jnp.where(s < last, 1, 0))

    def start_common():
        send("w", 0, 0, w1.at[o], w1o, partner)
        send("w", 1, 1, w2.at[o], w2o, partner)
        others(lambda b: send("tk", b, j, tok, tk.at[j], {"dp": b}))
        tk[j] = tok[...]

    def all_to_all(dst):
        others(lambda b: send("a", b, j, src.at[b * 2 + t], dst.at[t, blk(j)], {"dp": b}))
        dst[0, blk(j)] = src[j * 2]
        dst[1, blk(j)] = src[j * 2 + 1]

    def arrive(kind, fkind, buf, b):
        got(kind, b, buf.at[t, blk(b)])
        send(fkind, b, b, buf.at[t, blk(b)], buf.at[t, blk(b)], partner)
        got(fkind, b, buf.at[o, blk(b)])

    lane = lax.broadcasted_iota(jnp.int32, (rows, LANES), 1)

    def pack(values):
        packed = jnp.zeros((rows, LANES), F32)
        for i, value in enumerate(values):
            for half, part in enumerate(halves(value)):
                packed = jnp.where(lane == 2 * i + half, part.astype(F32), packed)
        return packed.astype(BF)

    def unpack(packed, i):
        return jnp.sum(
            jnp.where((lane == 2 * i) | (lane == 2 * i + 1), packed.astype(F32), 0.0),
            axis=1, keepdims=True,
        )

    def forward_chunk(b, with_logit):
        total = jnp.zeros((rows, v), F32)
        squares = jnp.zeros((rows, 1), F32)
        logit = jnp.zeros((rows, 1), F32)
        for h in range(2):
            x = xs[h, blk(b)].astype(F32)
            squares += jnp.sum(x * x, axis=1, keepdims=True)
            if with_logit:
                logit += jnp.sum(x * us[h, blk(b)].astype(F32), axis=1, keepdims=True)
            scaled = (x * gain[h]).astype(BF)
            xg[h, blk(b)] = scaled
            total += dot(scaled, w1[h])
        pb[blk(b), :v] = total.astype(BF)
        pb[blk(b), v:] = pack([squares, logit] if with_logit else [squares])

        @pl.when(b != j)
        def _():
            send("p", b, j, pb.at[blk(b)], pr.at[j], {"dp": b})

    def backward_chunk(b):
        total = dot(us[0, blk(b)], w2[0], 1, 1) + dot(us[1, blk(b)], w2[1], 1, 1)
        qb[blk(b)] = total.astype(BF)

        @pl.when(b != j)
        def _():
            send("q", b, j, qb.at[blk(b)], qr.at[j], {"dp": b})

    def reduce(kind, own, landed, acc):
        acc[...] = own[blk(j)].astype(F32)

        def add(b):
            got(kind, b, landed.at[b])
            acc[...] += landed[b].astype(F32)
        others(add)

    def share(kind, buf, forward):
        others(lambda b: send(kind, b, j, buf.at[t, blk(j)], buf.at[t, blk(j)], {"dp": b}))
        if forward:
            send(kind + "f", j, j, buf.at[t, blk(j)], buf.at[t, blk(j)], partner)

    def shared(kind, buf, b):
        @pl.when(b != j)
        def _():
            got(kind, b, buf.at[t, blk(b)])
            send(kind + "f", b, b, buf.at[t, blk(b)], buf.at[t, blk(b)], partner)
        got(kind + "f", b, buf.at[o, blk(b)])

    def own_inverse():
        inverse = lax.rsqrt(unpack(pacc[:, v:], 0) / width + eps_norm)
        rkeep[...] = jnp.broadcast_to(inverse, (rows, LANES))
        return inverse

    def forward_out():
        reduce("p", pb, pr, pacc)
        inverse = own_inverse()
        pj[t, blk(j)] = (inverse * pacc[:, :v]).astype(BF)
        share("pj", pj, True)
        got("w", 1, w2o)

        def chunk(b):
            shared("pj", pj, b)
            mixed = dot(pj[t, blk(b)], w2[t]) + dot(pj[o, blk(b)], w2o[...])
            yx[blk(b)] = (xs[t, blk(b)].astype(F32) + mixed).astype(BF)
            send("x", b, b, yx.at[blk(b)], xs.at[t, blk(b)], {"section": s + 1})
        everyone(chunk)

    def dot_over_units():
        exs[...] = jnp.broadcast_to(
            jnp.sum(pacc[:, :v] * qacc[...], axis=1, keepdims=True), (rows, LANES)
        )
        send("e", 0, 0, exs, exr, partner)
        got("e", 0, exr)
        return exs[:, :1] + exr[:, :1]

    def backward_out(is_last):
        reduce("q", qb, qr, qacc)
        inner = dot_over_units()
        inverse = rkeep[:, :1]
        if is_last:
            logit = unpack(pacc[:, v:], 1) + inverse * inner
            seed = rinfo[:, 0:1] * jnp.exp(logit - rinfo[:, 1:2])
            scale = seed * inverse
            pj[t, blk(j)] = (scale * pacc[:, :v]).astype(BF)
        else:
            seed = jnp.ones((rows, 1), F32)
            scale = inverse
        gq[t, blk(j)] = (scale * qacc[...]).astype(BF)
        sc[j] = pack([inverse * inverse * inverse * (seed * inner) / width, seed])
        share("gq", gq, True)
        others(lambda b: send("sc", b, j, sc.at[j], sc.at[j], {"dp": b}))
        if is_last:
            share("pj", pj, False)
        got("w", 0, w1o)

        def chunk(b):
            shared("gq", gq, b)

            @pl.when(b != j)
            def _():
                got("sc", b, sc.at[b])
            packed = sc[b]
            grad = dot(gq[t, blk(b)], w1[t], 1, 1) + dot(gq[o, blk(b)], w1o[...], 1, 1)
            upstream = us[t, blk(b)].astype(F32)
            if is_last:
                upstream = unpack(packed, 1) * upstream
            yg[blk(b)] = (
                upstream + gain[t] * grad - unpack(packed, 0) * xs[t, blk(b)].astype(F32)
            ).astype(BF)
            send("g", b, b, yg.at[blk(b)], us.at[t, blk(b)], {"section": s - 1})
        everyone(chunk)

    def tokens():
        count = tk[j]

        def add(b, total):
            return total
        others(lambda b: got("tk", b, tk.at[b]))
        count = tk[0]
        for b in range(1, n):
            count = count + tk[b]
        return 1.0 / count[0:1, 0:1]

    def finish_value(scale):
        for h in range(2):
            dw1[h] = dot(xg[h], gq[t], 0, 0) * scale

    def finish_output(scale):
        for h in range(2):
            dw2[h] = dot(pj[t], us[h], 0, 0) * scale

    def drain_common():
        sent("w", 0, w1o)
        sent("w", 1, w2o)

        def one(b):
            sent("tk", b, tk.at[b])
            sent("p", b, pb.at[blk(b)])
            sent("q", b, qb.at[blk(b)])
            sent("pj", b, pj.at[t, blk(b)])
            sent("gq", b, gq.at[t, blk(b)])
        others(one)

    def first_section():
        start_common()
        all_to_all(xs)
        forward_chunk(j, False)

        def chunk(b):
            arrive("a", "xf", xs, b)
            forward_chunk(b, False)
        others(chunk)
        forward_out()

        def back(b):
            arrive("g", "uf", us, b)
            backward_chunk(b)
        everyone(back)
        scale = tokens()
        reduce("q", qb, qr, qacc)
        gq[t, blk(j)] = (rkeep[:, :1] * qacc[...]).astype(BF)
        share("gq", gq, False)
        finish_output(scale)
        others(lambda b: got("gq", b, gq.at[t, blk(b)]))
        finish_value(scale)
        got("w", 0, w1o)
        drain_common()

        def rest(b):
            sent("a", b, src.at[0])
            sent("xf", b, xs.at[t, blk(b)])
        others(rest)

        def rest_all(b):
            sent("pjf", b, pj.at[t, blk(b)])
            sent("x", b, yx.at[blk(b)])
            sent("uf", b, us.at[t, blk(b)])
        everyone(rest_all)

    def middle_section():
        start_common()

        def chunk(b):
            arrive("x", "xf", xs, b)
            forward_chunk(b, False)
        everyone(chunk)
        forward_out()

        def back(b):
            arrive("g", "uf", us, b)
            backward_chunk(b)
        everyone(back)
        backward_out(False)
        scale = tokens()
        finish_output(scale)
        finish_value(scale)
        drain_common()
        sent("e", 0, exs)
        others(lambda b: sent("sc", b, sc.at[b]))

        def rest_all(b):
            sent("xf", b, xs.at[t, blk(b)])
            sent("uf", b, us.at[t, blk(b)])
            sent("pjf", b, pj.at[t, blk(b)])
            sent("gqf", b, gq.at[t, blk(b)])
            sent("x", b, yx.at[blk(b)])
            sent("g", b, yg.at[blk(b)])
        everyone(rest_all)

    def last_section():
        start_common()
        all_to_all(us)
        backward_chunk(j)

        def seeds(b):
            arrive("a", "uf", us, b)
            backward_chunk(b)
        others(seeds)

        def chunk(b):
            arrive("x", "xf", xs, b)
            forward_chunk(b, True)
        everyone(chunk)
        reduce("p", pb, pr, pacc)
        own_inverse()
        backward_out(True)
        scale = tokens()
        finish_value(scale)
        others(lambda b: got("pj", b, pj.at[t, blk(b)]))
        finish_output(scale)
        got("w", 1, w2o)
        drain_common()
        sent("e", 0, exs)

        def rest(b):
            sent("a", b, src.at[0])
            sent("uf", b, us.at[t, blk(b)])
            sent("sc", b, sc.at[b])
        others(rest)

        def rest_all(b):
            sent("xf", b, xs.at[t, blk(b)])
            sent("gqf", b, gq.at[t, blk(b)])
            sent("g", b, yg.at[blk(b)])
        everyone(rest_all)

    pl.when(s == 0)(first_section)
    pl.when(s == last)(last_section)
    if sections > 2:
        pl.when((s > 0) & (s < last))(middle_section)


def local(
    hidden, unembed, value_proj, output_proj, norm_gains, survive, lengths, assign,
    advantage, reference_logit, recorded_gap,
):
    n = lax.axis_size("dp")
    sections = lax.axis_size("section")
    j = lax.axis_index("dp")
    s = lax.axis_index("section")
    count, positions, width = hidden.shape
    rows = count * positions
    part = value_proj.shape[1]
    half = part // 2
    v = value_proj.shape[2]
    group = count // survive.shape[0]

    src = jnp.where(s == sections - 1, unembed, hidden).reshape(rows, n * 2, half)
    src = src.transpose(1, 0, 2)
    w1 = value_proj[0].reshape(2, half, v)
    w2 = output_proj[0].reshape(v, 2, half).transpose(1, 0, 2)
    gain = lax.dynamic_slice(norm_gains[0], (j * part,), (part,)).reshape(2, 1, half)
    present = jnp.sum(
        (assign[None, :] == jnp.arange(count, dtype=jnp.int32)[:, None]).astype(F32), axis=1
    )
    live = (
        lax.broadcasted_iota(jnp.int32, (count, positions), 1) < lengths[:, None]
    ).astype(F32)
    adv = advantage[:, None]
    clipped = ((adv > 0) & (recorded_gap > clip_high)) | ((adv < 0) & (recorded_gap < clip_low))
    weight = -loss_scale * adv * (1.0 - clipped.astype(F32)) * live * present[:, None]
    rinfo = jnp.stack([weight.reshape(rows), reference_logit.reshape(rows)], axis=1)
    tok = jnp.sum((jnp.repeat(survive, group) * lengths).astype(F32))
    tok = jnp.broadcast_to(tok, (8, LANES))

    total = n * rows
    kinds = len(KINDS)
    vm = pl.BlockSpec(memory_space=pltpu.VMEM)
    dw1, dw2 = pl.pallas_call(
        functools.partial(kernel, n, sections, width),
        out_shape=(
            jax.ShapeDtypeStruct((2, half, v), F32),
            jax.ShapeDtypeStruct((2, v, half), F32),
        ),
        in_specs=[vm] * 6,
        out_specs=(vm, vm),
        scratch_shapes=[
            pltpu.VMEM((2, total, half), BF),
            pltpu.VMEM((2, total, half), BF),
            pltpu.VMEM((2, total, half), BF),
            pltpu.VMEM((total, v + LANES), BF),
            pltpu.VMEM((n, rows, v + LANES), BF),
            pltpu.VMEM((total, v), BF),
            pltpu.VMEM((n, rows, v), BF),
            pltpu.VMEM((2, total, v), BF),
            pltpu.VMEM((2, total, v), BF),
            pltpu.VMEM((n, rows, LANES), BF),
            pltpu.VMEM((half, v), BF),
            pltpu.VMEM((v, half), BF),
            pltpu.VMEM((total, half), BF),
            pltpu.VMEM((total, half), BF),
            pltpu.VMEM((n, 8, LANES), F32),
            pltpu.VMEM((rows, LANES), F32),
            pltpu.VMEM((rows, LANES), F32),
            pltpu.VMEM((rows, v + LANES), F32),
            pltpu.VMEM((rows, v), F32),
            pltpu.VMEM((rows, LANES), F32),
            pltpu.SemaphoreType.DMA((kinds, n)),
            pltpu.SemaphoreType.DMA((kinds, n)),
        ],
        compiler_params=pltpu.CompilerParams(
            collective_id=0, has_side_effects=True, vmem_limit_bytes=60 * 1024 * 1024
        ),
    )(src, w1, w2, gain, rinfo, tok)
    return (
        dw1.reshape(1, part, v),
        dw2.transpose(1, 0, 2).reshape(1, v, part),
    )


def solution(mesh):
    rowwise = P(("groups", "dp"))
    placed = (
        P(("groups", "dp"), None, None),
        P(("groups", "dp"), None, None),
        P("section", "dp", "tensor"),
        P("section", "tensor", "dp"),
        P("section", None),
        rowwise,
        rowwise,
        rowwise,
        rowwise,
        P(("groups", "dp"), None),
        P(("groups", "dp"), None),
    )
    return jax.shard_map(
        local,
        mesh=mesh,
        in_specs=placed,
        out_specs=(
            P(("groups", "section"), "dp", "tensor"),
            P(("groups", "section"), "tensor", "dp"),
        ),
        check_vma=False,
    )
```

time: 450 us -> 114 us (0.25)
  waiting for transfers between devices: 326 us -> 0 us
  Pallas kernels: 0 us -> 96.5 us
  other arithmetic: 32.2 us -> 4.2 us
  local copies, waits for them, and re-layouts: 32.9 us -> 11.8 us
  matrix products: 19.3 us -> 0 us
  between operations: 15.3 us -> 1.37 us
  blocking collectives: 12.9 us -> 0 us
  starting transfers between devices: 10.5 us -> 0 us
    all_gather x2 -> x0, waiting for transfers between devices: 101 us -> none  [the longest x1 52.5 us: local(): lax.all_gather(output_proj, 'dp', axis=2, tiled=True)]
    pallas_call x0 -> x1, Pallas kernels: none -> 96.5 us  [local(): pl.pallas_call(functools.partial(kernel, n, sections, width), out_shape=(...]
    psum x5 -> x0, waiting for transfers between devices: 85.4 us -> none  [the longest x3 48.4 us: local(): lax.psum(partial_out.astype(jnp.bfloat16), 'tensor').astype(jnp.float32)]
    reduce_scatter x1 -> x0, waiting for transfers between devices: 80.2 us -> none  [local(): lax.psum_scatter(jnp.concatenate([contract_first(flat_normed, flat_grad_v...]
    ppermute x4 -> x0, waiting for transfers between devices: 57.8 us -> none  [from_behind(): return lax.ppermute(block, axis, route)]
    dot_general x13 -> x0, matrix products: 19.3 us -> none  [the longest x5 6.28 us: contract_last(): lax.dot_general(left_rows, right_rows, (((1,), (1,)), ((), ())), preferre...]
    dynamic_update_slice x10 -> x0, other arithmetic: 14.3 us -> none  [put_slot(): lax.dynamic_update_index_in_dim(slot_store, jnp.where(active, new_value,...]
    psum x1 -> x0, blocking collectives: 12.9 us -> none  [local(): token_total = lax.psum(local_count, 'dp')]
  transfers between devices with their start and end apart: 12 -> 0, of which waited for: 12 -> 0; matrix products, arithmetic and copies ran while one was open for 6% -> 0% of each run, Pallas kernels for 0% -> 0%
where the time goes in v1:
time: 114 us
  Pallas kernels  96.5 us (85%)
  local copies, waits for them, and re-layouts  11.8 us (10%)
  other arithmetic  4.2 us (4%)
  between operations  1.37 us (1%)
    pallas_call x1, Pallas kernels, local(): pl.pallas_call(functools.partial(kernel, n, sections, width), out_shape=(...  96.5 us
    unnamed x13, local copies, waits for them, and re-layouts  4.97 us

profile of v1, /device:TPU:0, one launch (start us, length us, event | category | flops | bytes accessed | tf_op | source)
XLA Modules:
  0.0 113.9 jit_solution(12484245289016940394)
XLA Ops:
  0.6 0.0 copy-start
  1.3 1.3 %convert_reduce_fusion.1 = f32[]{:T(128)} fusion(s32[16]{0:T(128)} %param.17, s32[]{:T(128)} %bitcast.14), kind=kLoop, calls=%fused_computation.7 | loop fusion | flops 47 | bytes 72 | tf_op jit(solution)/shard_map/reduce_sum | solution.py:415
  2.6 0.8 convert_reduce_fusion
  3.3 0.7 broadcast_multiply_fusion
  4.0 0.7 broadcast_compare_fusion.1
  4.7 0.7 select_multiply_fusion
  5.4 1.2 %broadcast_in_dim.2.tok = f32[8,128]{1,0:T(8,128)} broadcast(f32[]{:T(128)} %convert_reduce_fusion.1), dimensions={} | broadcast | bytes 4100 | tf_op jit(solution)/shard_map/broadcast_in_dim | solution.py:416
  6.6 0.1 copy.37
  6.7 0.1 stack_reshape.6
  6.8 0.0 copy-done
  6.8 0.6 constant_dynamic-slice_fusion
  7.4 0.8 copy.38
  8.1 0.1 stack_reshape.7
  8.2 0.7 copy.39.rinfo
  9.0 0.0 copy-start.1
  9.0 0.0 copy-start.2
  9.0 1.5 %copy.35 = bf16[1,256,1280]{1,2,0:T(8,128)(2,1)S(1)} copy(bf16[1,256,1280]{2,1,0:T(8,128)(2,1)} %param.14) | data formatting | bytes 1310720 | tf_op args[3]
  10.5 1.1 copy.36
  11.5 0.0 copy-done.1
  11.5 0.0 copy-done.2
  11.5 0.1 broadcast_select_fusion
  11.7 0.2 copy.42
  11.9 1.2 %copy.44 = bf16[128,8,640]{2,0,1:T(8,128)(2,1)} copy(bf16[128,8,640]{2,1,0:T(8,128)(2,1)S(1)} %bitcast.17) | data formatting | bytes 2621440 | tf_op jit(solution)/shard_map/reshape | solution.py:400
  13.1 96.5 %shard_map.125 = (f32[2,640,256]{2,1,0:T(8,128)}, f32[2,256,640]{2,1,0:T(8,128)}) custom-call(bf16[8,128,640]{2,1,0:T(8,128)(2,1)} %bitcast.15, bf16[2,640,256]{2,1,0:T(8,128)(2,1)} %bitcast.23, bf16[2,256,640]{2,1,0:T(8,128)(2,1)} %bitcast.20, f32[2,1,640]{2,1,0:T(1,128)} %bitcast.24, f32[128,2]{1,0:T(8,128)} %copy.39.rinfo, f32[8,128]{1,0:T(8,128)} %broadcast_in_dim.2.tok), custom_call_target="tpu_custom_call" | custom-call | tf_op jit(solution)/shard_map/pallas_call | solution.py:421
  109.6 1.7 %copy.40 = f32[256,2,640]{0,2,1:T(8,128)S(1)} copy(f32[256,2,640]{2,0,1:T(8,128)} %bitcast.22) | data formatting | bytes 2621440 | tf_op jit(solution)/shard_map/transpose | solution.py:459
  111.3 0.0 copy-start.3
  111.3 1.5 %copy.41 = f32[1,256,1280]{2,1,0:T(8,128)} copy(f32[1,256,1280]{1,2,0:T(8,128)S(1)} %bitcast.18) | data formatting | bytes 2621440
  112.8 0.0 copy-done.3
  112.8 1.1 copy.47
  (1 shorter events, 0.0 us)
Async XLA Ops:
  0.6 6.1 %copy-start = (f32[1,5120]{1,0:T(1,128)S(1)}, f32[1,5120]{1,0:T(1,128)}, u32[]{:S(2)}) copy-start(f32[1,5120]{1,0:T(1,128)} %param.15) | copy-start | bytes 61444
  9.0 2.6 %copy-start.1 = (bf16[16,8,5120]{2,1,0:T(8,128)(2,1)S(1)}, bf16[16,8,5120]{2,1,0:T(8,128)(2,1)}, u32[]{:S(2)}) copy-start(bf16[16,8,5120]{2,1,0:T(8,128)(2,1)} %param.12) | copy-start | bytes 3932164
  9.0 2.6 %copy-start.2 = (bf16[16,8,5120]{2,1,0:T(8,128)(2,1)S(1)}, bf16[16,8,5120]{2,1,0:T(8,128)(2,1)}, u32[]{:S(2)}) copy-start(bf16[16,8,5120]{2,1,0:T(8,128)(2,1)} %param.11) | copy-start | bytes 3932164
  111.3 1.5 %copy-start.3 = (f32[2,640,256]{2,1,0:T(8,128)S(1)}, f32[2,640,256]{2,1,0:T(8,128)}, u32[]{:S(2)}) copy-start(f32[2,640,256]{2,1,0:T(8,128)} %get-tuple-element.4) | copy-start | bytes 3932164

commit v2 on v1

--- a/solution.py
+++ b/solution.py
@@ -13,7 +13,7 @@
 clip_high = math.log(1.28)
 clip_low = math.log(0.8)
 LANES = 128
-KINDS = ("a", "xf", "uf", "p", "q", "pj", "pjf", "gq", "gqf", "sc", "tk", "x", "g", "w", "e")
+KINDS = ("a", "xf", "uf", "p", "q", "pj", "pjf", "gq", "gqf", "sc", "tk", "x", "g", "w", "e", "ps")
 BF = jnp.bfloat16
 F32 = jnp.float32
 
@@ -22,16 +22,12 @@
     return lax.dot_general(a, b, (((ca,), (cb,)), ((), ())), preferred_element_type=F32)
 
 
-def halves(value):
-    high = value.astype(BF)
-    return high, (value - high.astype(F32)).astype(BF)
-
-
 def kernel(
     n, sections, width,
-    src, w1, w2, gain, rinfo, tok,
+    src, w1, w2, gains, survive, lengths, assign, advantage, base, gap,
     dw1, dw2,
     xs, us, xg, pb, pr, qb, qr, pj, gq, sc, w1o, w2o, yx, yg, tk, exs, exr, pacc, qacc, rkeep,
+    ps, psr, rinfo, tok,
     ss, rs,
 ):
     j = lax.axis_index("dp")
@@ -42,6 +38,49 @@
     v = w1.shape[2]
     last = sections - 1
     partner = {"tensor": o}
+    count, positions = base.shape
+
+    def gain(h):
+        return gains[j * 2 + h]
+
+    def own_tokens():
+        response = lax.broadcasted_iota(jnp.int32, (1, count), 1)
+        group = count // survive.shape[1]
+        kept = jnp.zeros((1, count), F32)
+        for g in range(survive.shape[1]):
+            inside = (response >= g * group) & (response < (g + 1) * group)
+            kept = jnp.where(inside, survive[0:1, g:g + 1].astype(F32), kept)
+        held = jnp.sum(kept * lengths[...].astype(F32), axis=1, keepdims=True)
+        tok[...] = jnp.broadcast_to(held, (8, LANES))
+
+    def row_info():
+        row = lax.broadcasted_iota(jnp.int32, (rows, count), 0)
+        first = lax.broadcasted_iota(jnp.int32, (rows, count), 1) * positions
+        mine = (row >= first) & (row < first + positions)
+        diagonal = lax.broadcasted_iota(jnp.int32, (count, positions, positions), 1)
+        diagonal = diagonal == lax.broadcasted_iota(
+            jnp.int32, (count, positions, positions), 2
+        )
+
+        def by_response(values):
+            return jnp.sum(jnp.where(mine, values, 0.0), axis=1, keepdims=True)
+
+        def by_position(values):
+            spread = jnp.where(diagonal, values[:, None, :], 0.0)
+            return jnp.sum(spread, axis=2, keepdims=True).reshape(rows, 1)
+
+        slots = assign[...]
+        starts = slots * positions
+        hit = (row >= starts) & (row < starts + positions)
+        listed = jnp.sum(jnp.where(hit, 1.0, 0.0), axis=1, keepdims=True)
+        start = by_response(first.astype(F32))
+        place = lax.broadcasted_iota(jnp.int32, (rows, 1), 0).astype(F32) - start
+        live = place < by_response(lengths[...].astype(F32))
+        adv = by_response(advantage[...])
+        q = by_position(gap[...])
+        clipped = ((adv > 0) & (q > clip_high)) | ((adv < 0) & (q < clip_low))
+        weight = jnp.where(clipped | (~live), 0.0, -loss_scale * adv * listed)
+        rinfo[...] = jnp.where(lane == 0, weight, jnp.where(lane == 1, by_position(base[...]), 0.0))
 
     def blk(b):
         return pl.ds(pl.multiple_of(b * rows, rows), rows)
@@ -103,6 +142,7 @@
     def start_common():
         send("w", 0, 0, w1.at[o], w1o, partner)
         send("w", 1, 1, w2.at[o], w2o, partner)
+        own_tokens()
         others(lambda b: send("tk", b, j, tok, tk.at[j], {"dp": b}))
         tk[j] = tok[...]
 
@@ -121,15 +161,12 @@
     def pack(values):
         packed = jnp.zeros((rows, LANES), F32)
         for i, value in enumerate(values):
-            for half, part in enumerate(halves(value)):
-                packed = jnp.where(lane == 2 * i + half, part.astype(F32), packed)
-        return packed.astype(BF)
-
-    def unpack(packed, i):
-        return jnp.sum(
-            jnp.where((lane == 2 * i) | (lane == 2 * i + 1), packed.astype(F32), 0.0),
-            axis=1, keepdims=True,
-        )
+            packed = jnp.where(lane == i, value, packed)
+        return packed.T[:8]
+
+    def unpack(packed):
+        filled = jnp.concatenate([packed, jnp.zeros((LANES - 8, rows), F32)], axis=0)
+        return filled.T
 
     def forward_chunk(b, with_logit):
         total = jnp.zeros((rows, v), F32)
@@ -140,15 +177,16 @@
             squares += jnp.sum(x * x, axis=1, keepdims=True)
             if with_logit:
                 logit += jnp.sum(x * us[h, blk(b)].astype(F32), axis=1, keepdims=True)
-            scaled = (x * gain[h]).astype(BF)
+            scaled = (x * gain(h)).astype(BF)
             xg[h, blk(b)] = scaled
             total += dot(scaled, w1[h])
-        pb[blk(b), :v] = total.astype(BF)
-        pb[blk(b), v:] = pack([squares, logit] if with_logit else [squares])
+        pb[blk(b)] = total.astype(BF)
+        ps[b] = pack([squares, logit] if with_logit else [squares])
 
         @pl.when(b != j)
         def _():
             send("p", b, j, pb.at[blk(b)], pr.at[j], {"dp": b})
+            send("ps", b, j, ps.at[b], psr.at[j], {"dp": b})
 
     def backward_chunk(b):
         total = dot(us[0, blk(b)], w2[0], 1, 1) + dot(us[1, blk(b)], w2[1], 1, 1)
@@ -179,14 +217,20 @@
         got(kind + "f", b, buf.at[o, blk(b)])
 
     def own_inverse():
-        inverse = lax.rsqrt(unpack(pacc[:, v:], 0) / width + eps_norm)
-        rkeep[...] = jnp.broadcast_to(inverse, (rows, LANES))
+        psr[j] = ps[j]
+        others(lambda b: got("ps", b, psr.at[b]))
+        sums = psr[0]
+        for b in range(1, n):
+            sums = sums + psr[b]
+        sums = unpack(sums)
+        inverse = lax.rsqrt(sums[:, 0:1] / width + eps_norm)
+        rkeep[...] = jnp.where(lane == 0, inverse, sums)
         return inverse
 
     def forward_out():
+        inverse = own_inverse()
         reduce("p", pb, pr, pacc)
-        inverse = own_inverse()
-        pj[t, blk(j)] = (inverse * pacc[:, :v]).astype(BF)
+        pj[t, blk(j)] = (inverse * pacc[...]).astype(BF)
         share("pj", pj, True)
         got("w", 1, w2o)
 
@@ -199,7 +243,7 @@
 
     def dot_over_units():
         exs[...] = jnp.broadcast_to(
-            jnp.sum(pacc[:, :v] * qacc[...], axis=1, keepdims=True), (rows, LANES)
+            jnp.sum(pacc[...] * qacc[...], axis=1, keepdims=True), (rows, LANES)
         )
         send("e", 0, 0, exs, exr, partner)
         got("e", 0, exr)
@@ -210,10 +254,10 @@
         inner = dot_over_units()
         inverse = rkeep[:, :1]
         if is_last:
-            logit = unpack(pacc[:, v:], 1) + inverse * inner
+            logit = rkeep[:, 1:2] + inverse * inner
             seed = rinfo[:, 0:1] * jnp.exp(logit - rinfo[:, 1:2])
             scale = seed * inverse
-            pj[t, blk(j)] = (scale * pacc[:, :v]).astype(BF)
+            pj[t, blk(j)] = (scale * pacc[...]).astype(BF)
         else:
             seed = jnp.ones((rows, 1), F32)
             scale = inverse
@@ -221,8 +265,6 @@
         sc[j] = pack([inverse * inverse * inverse * (seed * inner) / width, seed])
         share("gq", gq, True)
         others(lambda b: send("sc", b, j, sc.at[j], sc.at[j], {"dp": b}))
-        if is_last:
-            share("pj", pj, False)
         got("w", 0, w1o)
 
         def chunk(b):
@@ -231,22 +273,18 @@
             @pl.when(b != j)
             def _():
                 got("sc", b, sc.at[b])
-            packed = sc[b]
+            packed = unpack(sc[b])
             grad = dot(gq[t, blk(b)], w1[t], 1, 1) + dot(gq[o, blk(b)], w1o[...], 1, 1)
             upstream = us[t, blk(b)].astype(F32)
             if is_last:
-                upstream = unpack(packed, 1) * upstream
+                upstream = packed[:, 1:2] * upstream
             yg[blk(b)] = (
-                upstream + gain[t] * grad - unpack(packed, 0) * xs[t, blk(b)].astype(F32)
+                upstream + gain(t) * grad - packed[:, 0:1] * xs[t, blk(b)].astype(F32)
             ).astype(BF)
             send("g", b, b, yg.at[blk(b)], us.at[t, blk(b)], {"section": s - 1})
         everyone(chunk)
 
     def tokens():
-        count = tk[j]
-
-        def add(b, total):
-            return total
         others(lambda b: got("tk", b, tk.at[b]))
         count = tk[0]
         for b in range(1, n):
@@ -257,6 +295,18 @@
         for h in range(2):
             dw1[h] = dot(xg[h], gq[t], 0, 0) * scale
 
+    def finish_value_arriving(scale):
+        def add(b, start):
+            for h in range(2):
+                part = dot(xg[h, blk(b)], gq[t, blk(b)], 0, 0) * scale
+                dw1[h] = part if start else dw1[h] + part
+        add(j, True)
+
+        def later(b):
+            got("gq", b, gq.at[t, blk(b)])
+            add(b, False)
+        others(later)
+
     def finish_output(scale):
         for h in range(2):
             dw2[h] = dot(pj[t], us[h], 0, 0) * scale
@@ -268,6 +318,7 @@
         def one(b):
             sent("tk", b, tk.at[b])
             sent("p", b, pb.at[blk(b)])
+            sent("ps", b, ps.at[b])
             sent("q", b, qb.at[blk(b)])
             sent("pj", b, pj.at[t, blk(b)])
             sent("gq", b, gq.at[t, blk(b)])
@@ -293,8 +344,7 @@
         gq[t, blk(j)] = (rkeep[:, :1] * qacc[...]).astype(BF)
         share("gq", gq, False)
         finish_output(scale)
-        others(lambda b: got("gq", b, gq.at[t, blk(b)]))
-        finish_value(scale)
+        finish_value_arriving(scale)
         got("w", 0, w1o)
         drain_common()
 
@@ -343,6 +393,7 @@
         start_common()
         all_to_all(us)
         backward_chunk(j)
+        row_info()
 
         def seeds(b):
             arrive("a", "uf", us, b)
@@ -353,9 +404,10 @@
             arrive("x", "xf", xs, b)
             forward_chunk(b, True)
         everyone(chunk)
+        own_inverse()
         reduce("p", pb, pr, pacc)
-        own_inverse()
         backward_out(True)
+        share("pj", pj, False)
         scale = tokens()
         finish_value(scale)
         others(lambda b: got("pj", b, pj.at[t, blk(b)]))
@@ -388,33 +440,18 @@
 ):
     n = lax.axis_size("dp")
     sections = lax.axis_size("section")
-    j = lax.axis_index("dp")
     s = lax.axis_index("section")
     count, positions, width = hidden.shape
     rows = count * positions
     part = value_proj.shape[1]
     half = part // 2
     v = value_proj.shape[2]
-    group = count // survive.shape[0]
 
     src = jnp.where(s == sections - 1, unembed, hidden).reshape(rows, n * 2, half)
     src = src.transpose(1, 0, 2)
     w1 = value_proj[0].reshape(2, half, v)
     w2 = output_proj[0].reshape(v, 2, half).transpose(1, 0, 2)
-    gain = lax.dynamic_slice(norm_gains[0], (j * part,), (part,)).reshape(2, 1, half)
-    present = jnp.sum(
-        (assign[None, :] == jnp.arange(count, dtype=jnp.int32)[:, None]).astype(F32), axis=1
-    )
-    live = (
-        lax.broadcasted_iota(jnp.int32, (count, positions), 1) < lengths[:, None]
-    ).astype(F32)
-    adv = advantage[:, None]
-    clipped = ((adv > 0) & (recorded_gap > clip_high)) | ((adv < 0) & (recorded_gap < clip_low))
-    weight = -loss_scale * adv * (1.0 - clipped.astype(F32)) * live * present[:, None]
-    rinfo = jnp.stack([weight.reshape(rows), reference_logit.reshape(rows)], axis=1)
-    tok = jnp.sum((jnp.repeat(survive, group) * lengths).astype(F32))
-    tok = jnp.broadcast_to(tok, (8, LANES))
-
+    gains = norm_gains[0].reshape(n * 2, 1, half)
     total = n * rows
     kinds = len(KINDS)
     vm = pl.BlockSpec(memory_space=pltpu.VMEM)
@@ -424,19 +461,19 @@
             jax.ShapeDtypeStruct((2, half, v), F32),
             jax.ShapeDtypeStruct((2, v, half), F32),
         ),
-        in_specs=[vm] * 6,
+        in_specs=[vm] * 10,
         out_specs=(vm, vm),
         scratch_shapes=[
             pltpu.VMEM((2, total, half), BF),
             pltpu.VMEM((2, total, half), BF),
             pltpu.VMEM((2, total, half), BF),
-            pltpu.VMEM((total, v + LANES), BF),
-            pltpu.VMEM((n, rows, v + LANES), BF),
+            pltpu.VMEM((total, v), BF),
+            pltpu.VMEM((n, rows, v), BF),
             pltpu.VMEM((total, v), BF),
             pltpu.VMEM((n, rows, v), BF),
             pltpu.VMEM((2, total, v), BF),
             pltpu.VMEM((2, total, v), BF),
-            pltpu.VMEM((n, rows, LANES), BF),
+            pltpu.VMEM((n, 8, rows), F32),
             pltpu.VMEM((half, v), BF),
             pltpu.VMEM((v, half), BF),
             pltpu.VMEM((total, half), BF),
@@ -444,16 +481,23 @@
             pltpu.VMEM((n, 8, LANES), F32),
             pltpu.VMEM((rows, LANES), F32),
             pltpu.VMEM((rows, LANES), F32),
-            pltpu.VMEM((rows, v + LANES), F32),
+            pltpu.VMEM((rows, v), F32),
             pltpu.VMEM((rows, v), F32),
             pltpu.VMEM((rows, LANES), F32),
+            pltpu.VMEM((n, 8, rows), F32),
+            pltpu.VMEM((n, 8, rows), F32),
+            pltpu.VMEM((rows, LANES), F32),
+            pltpu.VMEM((8, LANES), F32),
             pltpu.SemaphoreType.DMA((kinds, n)),
             pltpu.SemaphoreType.DMA((kinds, n)),
         ],
         compiler_params=pltpu.CompilerParams(
             collective_id=0, has_side_effects=True, vmem_limit_bytes=60 * 1024 * 1024
         ),
-    )(src, w1, w2, gain, rinfo, tok)
+    )(
+        src, w1, w2, gains, survive.reshape(1, -1), lengths.reshape(1, count),
+        assign.reshape(1, count), advantage.reshape(1, count), reference_logit, recorded_gap,
+    )
     return (
         dw1.reshape(1, part, v),
         dw2.transpose(1, 0, 2).reshape(1, v, part),

time: 114 us -> 104 us (0.912)
  Pallas kernels: 96.5 us -> 91.1 us
  other arithmetic: 4.2 us -> 0.14 us
    pallas_call x1, Pallas kernels: 96.5 us -> 91.1 us  [local(): pl.pallas_call(functools.partial(kernel, n, sections, width), out_shape=(...]
    reduce_sum x2 -> x0, other arithmetic: 2.03 us -> none  [the longest x1 1.26 us: local(): tok = jnp.sum((jnp.repeat(survive, group) * lengths).astype(F32))]
    unnamed x13 -> x12, local copies, waits for them, and re-layouts: 4.97 us -> 6.91 us
    mul x2 -> x0, other arithmetic: 1.36 us -> none  [local(): -loss_scale * adv * (1.0 - clipped.astype(F32)) * live * present[:, None]]
    broadcast_in_dim x1 -> x0, local copies, waits for them, and re-layouts: 1.24 us -> none  [local(): tok = jnp.broadcast_to(tok, (8, LANES))]
where the time goes in v2:
time: 104 us; the launch traced here: 103 us
  Pallas kernels  91.1 us (88%)
  local copies, waits for them, and re-layouts  10.9 us (10%)
  between operations  1.32 us (1%)
    pallas_call x1, Pallas kernels, local(): pl.pallas_call(functools.partial(kernel, n, sections, width), out_shape=(...  91.1 us
    unnamed x12, local copies, waits for them, and re-layouts  6.91 us

profile of v2, /device:TPU:0, one launch (start us, length us, event | category | flops | bytes accessed | tf_op | source)
XLA Modules:
  0.0 103.5 jit_solution(1184917252051129244)
XLA Ops:
  1.3 1.4 %copy.18.base = f32[16,8]{1,0:T(8,128)} copy(f32[16,8]{0,1:T(8,128)} %param.20) | data formatting | bytes 1024 | tf_op args[9]
  2.6 1.4 %copy.19.gap = f32[16,8]{1,0:T(8,128)} copy(f32[16,8]{0,1:T(8,128)} %param.21) | data formatting | bytes 1024 | tf_op args[10]
  4.0 0.0 copy-start
  4.0 0.0 copy-start.1
  4.0 1.5 %copy.16 = bf16[1,256,1280]{1,2,0:T(8,128)(2,1)S(1)} copy(bf16[1,256,1280]{2,1,0:T(8,128)(2,1)} %param.14) | data formatting | bytes 1310720 | tf_op args[3]
  5.5 1.1 %copy.17 = bf16[256,2,640]{2,0,1:T(8,128)(2,1)} copy(bf16[256,2,640]{0,2,1:T(8,128)(2,1)S(1)} %bitcast.22) | data formatting | bytes 1310720 | tf_op jit(solution)/shard_map/reshape;squeeze | solution.py:453
  6.5 0.0 copy-done
  6.5 0.0 copy-done.1
  6.5 0.1 broadcast_select_fusion
  6.7 0.2 copy.22
  6.9 1.2 %copy.24 = bf16[128,8,640]{2,0,1:T(8,128)(2,1)} copy(bf16[128,8,640]{2,1,0:T(8,128)(2,1)S(1)} %bitcast.20) | data formatting | bytes 2621440 | tf_op jit(solution)/shard_map/reshape | solution.py:450
  8.1 91.1 %shard_map.122 = (f32[2,640,256]{2,1,0:T(8,128)}, f32[2,256,640]{2,1,0:T(8,128)}) custom-call(bf16[8,128,640]{2,1,0:T(8,128)(2,1)} %bitcast.18, bf16[2,640,256]{2,1,0:T(8,128)(2,1)} %bitcast.26, bf16[2,256,640]{2,1,0:T(8,128)(2,1)} %bitcast.23, f32[8,1,640]{2,1,0:T(1,128)} %bitcast.27, s32[1,1]{1,0:T(1,128)} %bitcast.17.survive, s32[1,16]{1,0:T(1,128)} %bitcast.28, ...), custom_call_target="tpu_custom_call" | custom-call | tf_op jit(solution)/shard_map/pallas_call | solution.py:458
  99.2 1.7 %copy.20 = f32[256,2,640]{0,2,1:T(8,128)S(1)} copy(f32[256,2,640]{2,0,1:T(8,128)} %bitcast.25) | data formatting | bytes 2621440 | tf_op jit(solution)/shard_map/transpose | solution.py:503
  101.0 0.0 copy-start.2
  101.0 1.5 %copy.21 = f32[1,256,1280]{2,1,0:T(8,128)} copy(f32[1,256,1280]{1,2,0:T(8,128)S(1)} %bitcast.21) | data formatting | bytes 2621440
  102.4 0.0 copy-done.2
  102.4 1.1 %copy.27 = f32[1,1280,256]{2,1,0:T(8,128)} copy(f32[1,1280,256]{2,1,0:T(8,128)S(1)} %bitcast.24) | data formatting | bytes 2621440
Async XLA Ops:
  4.0 2.6 %copy-start = (bf16[16,8,5120]{2,1,0:T(8,128)(2,1)S(1)}, bf16[16,8,5120]{2,1,0:T(8,128)(2,1)}, u32[]{:S(2)}) copy-start(bf16[16,8,5120]{2,1,0:T(8,128)(2,1)} %param.12) | copy-start | bytes 3932164
  4.0 2.6 %copy-start.1 = (bf16[16,8,5120]{2,1,0:T(8,128)(2,1)S(1)}, bf16[16,8,5120]{2,1,0:T(8,128)(2,1)}, u32[]{:S(2)}) copy-start(bf16[16,8,5120]{2,1,0:T(8,128)(2,1)} %param.11) | copy-start | bytes 3932164
  101.0 1.5 %copy-start.2 = (f32[2,640,256]{2,1,0:T(8,128)S(1)}, f32[2,640,256]{2,1,0:T(8,128)}, u32[]{:S(2)}) copy-start(f32[2,640,256]{2,1,0:T(8,128)} %get-tuple-element.4) | copy-start | bytes 3932164

commit v3 on v2

--- a/solution.py
+++ b/solution.py
@@ -35,10 +35,10 @@
     t = lax.axis_index("tensor")
     o = 1 - t
     rows = src.shape[1]
-    v = w1.shape[2]
+    half, v = w1.shape[1:]
     last = sections - 1
     partner = {"tensor": o}
-    count, positions = base.shape
+    positions, count = base.shape
 
     def gain(h):
         return gains[j * 2 + h]
@@ -57,17 +57,12 @@
         row = lax.broadcasted_iota(jnp.int32, (rows, count), 0)
         first = lax.broadcasted_iota(jnp.int32, (rows, count), 1) * positions
         mine = (row >= first) & (row < first + positions)
-        diagonal = lax.broadcasted_iota(jnp.int32, (count, positions, positions), 1)
-        diagonal = diagonal == lax.broadcasted_iota(
-            jnp.int32, (count, positions, positions), 2
-        )
 
         def by_response(values):
             return jnp.sum(jnp.where(mine, values, 0.0), axis=1, keepdims=True)
 
         def by_position(values):
-            spread = jnp.where(diagonal, values[:, None, :], 0.0)
-            return jnp.sum(spread, axis=2, keepdims=True).reshape(rows, 1)
+            return by_response(jnp.concatenate([values] * count, axis=0))
 
         slots = assign[...]
         starts = slots * positions
@@ -309,7 +304,7 @@
 
     def finish_output(scale):
         for h in range(2):
-            dw2[h] = dot(pj[t], us[h], 0, 0) * scale
+            dw2[:, h * half:(h + 1) * half] = dot(pj[t], us[h], 0, 0) * scale
 
     def drain_common():
         sent("w", 0, w1o)
@@ -459,7 +454,7 @@
         functools.partial(kernel, n, sections, width),
         out_shape=(
             jax.ShapeDtypeStruct((2, half, v), F32),
-            jax.ShapeDtypeStruct((2, v, half), F32),
+            jax.ShapeDtypeStruct((v, part), F32),
         ),
         in_specs=[vm] * 10,
         out_specs=(vm, vm),
@@ -496,11 +491,11 @@
         ),
     )(
         src, w1, w2, gains, survive.reshape(1, -1), lengths.reshape(1, count),
-        assign.reshape(1, count), advantage.reshape(1, count), reference_logit, recorded_gap,
+        assign.reshape(1, count), advantage.reshape(1, count), reference_logit.T, recorded_gap.T,
     )
     return (
         dw1.reshape(1, part, v),
-        dw2.transpose(1, 0, 2).reshape(1, v, part),
+        dw2[None],
     )
 
 

time: 104 us -> 100 us (0.962)
  local copies, waits for them, and re-layouts: 10.9 us -> 7.6 us
    transpose x1 -> x0, local copies, waits for them, and re-layouts: 1.71 us -> none  [local(): return (dw1.reshape(1, part, v), dw2.transpose(1, 0, 2).reshape(1, v, part))]
    unnamed x12 -> x10, local copies, waits for them, and re-layouts: 6.91 us -> 5.31 us
where the time goes in v3:
time: 100 us
  Pallas kernels  91.1 us (91%)
  local copies, waits for them, and re-layouts  7.6 us (8%)
  between operations  1.33 us (1%)
    pallas_call x1, Pallas kernels, local(): pl.pallas_call(functools.partial(kernel, n, sections, width), out_shape=(...  91.1 us
    unnamed x10, local copies, waits for them, and re-layouts  5.31 us

profile of v3, /device:TPU:0, one launch (start us, length us, event | category | flops | bytes accessed | tf_op | source)
XLA Modules:
  0.0 100.2 jit_solution(4252063793616444441)
XLA Ops:
  1.3 0.0 copy-start
  1.3 0.0 copy-start.1
  1.3 1.5 %copy.14 = bf16[1,256,1280]{1,2,0:T(8,128)(2,1)S(1)} copy(bf16[1,256,1280]{2,1,0:T(8,128)(2,1)} %param.14) | data formatting | bytes 1310720 | tf_op args[3]
  2.8 1.1 %copy.15 = bf16[256,2,640]{2,0,1:T(8,128)(2,1)} copy(bf16[256,2,640]{0,2,1:T(8,128)(2,1)S(1)} %bitcast.22) | data formatting | bytes 1310720 | tf_op jit(solution)/shard_map/reshape;squeeze | solution.py:448
  3.9 0.0 copy-done
  3.9 0.0 copy-done.1
  3.9 0.1 broadcast_select_fusion
  4.0 0.2 copy.16
  4.2 1.2 %copy.18 = bf16[128,8,640]{2,0,1:T(8,128)(2,1)} copy(bf16[128,8,640]{2,1,0:T(8,128)(2,1)S(1)} %bitcast.21) | data formatting | bytes 2621440 | tf_op jit(solution)/shard_map/reshape | solution.py:445
  5.4 91.1 %shard_map.122 = (f32[2,640,256]{2,1,0:T(8,128)}, f32[256,1280]{1,0:T(8,128)}) custom-call(bf16[8,128,640]{2,1,0:T(8,128)(2,1)} %bitcast.19, bf16[2,640,256]{2,1,0:T(8,128)(2,1)} %bitcast.26, bf16[2,256,640]{2,1,0:T(8,128)(2,1)} %bitcast.23, f32[8,1,640]{2,1,0:T(1,128)} %bitcast.27, s32[1,1]{1,0:T(1,128)} %bitcast.18.survive, s32[1,16]{1,0:T(1,128)} %bitcast.30, ...), custom_call_target="tpu_custom_call" | custom-call | tf_op jit(solution)/shard_map/pallas_call | solution.py:453
  96.5 0.0 copy-start.2
  96.6 2.6 %copy.22 = f32[1,1280,256]{2,1,0:T(8,128)} copy(f32[1,1280,256]{2,1,0:T(8,128)} %bitcast.25) | data formatting | bytes 2621440
  99.1 0.0 copy-done.2
  99.1 1.1 %copy.23 = f32[1,256,1280]{2,1,0:T(8,128)} copy(f32[1,256,1280]{2,1,0:T(8,128)S(1)} %bitcast.24) | data formatting | bytes 2621440
Async XLA Ops:
  1.3 2.6 %copy-start = (bf16[16,8,5120]{2,1,0:T(8,128)(2,1)S(1)}, bf16[16,8,5120]{2,1,0:T(8,128)(2,1)}, u32[]{:S(2)}) copy-start(bf16[16,8,5120]{2,1,0:T(8,128)(2,1)} %param.12) | copy-start | bytes 3932164
  1.3 2.6 %copy-start.1 = (bf16[16,8,5120]{2,1,0:T(8,128)(2,1)S(1)}, bf16[16,8,5120]{2,1,0:T(8,128)(2,1)}, u32[]{:S(2)}) copy-start(bf16[16,8,5120]{2,1,0:T(8,128)(2,1)} %param.11) | copy-start | bytes 3932164
  96.5 2.6 %copy-start.2 = (f32[256,1280]{1,0:T(8,128)S(1)}, f32[256,1280]{1,0:T(8,128)}, u32[]{:S(2)}) copy-start(f32[256,1280]{1,0:T(8,128)} %get-tuple-element.5) | copy-start | bytes 3932164
